TPU v7x, 8 devices: a whole 2x2x1 slice. The times are simulated.
8 devices in a mesh: fsdp: 8 (over z, y, x, core).
Axes of the slice: x: 2, y: 2, z: 1, core: 2. Of those that a mesh axis runs over, the one named last changes fastest.
Arguments:
- patches: bfloat16 [64, 196, 768], P('fsdp')
- keep: int32 [64, 98], P('fsdp')
- w_patch: float32 [768, 384], P(None, 'fsdp')
- b_patch: float32 [384], P('fsdp')
- pos_table: float32 [197, 384], P(None, 'fsdp')
- cls_tok: float32 [384], P('fsdp')
- lnp_g: float32 [384], P('fsdp')
- lnp_b: float32 [384], P('fsdp')
- ln1_g: float32 [384], P('fsdp')
- ln1_b: float32 [384], P('fsdp')
- w_qkv: float32 [384, 3, 6, 64], P('fsdp')
- b_qkv: float32 [1152], P('fsdp')
- w_out: float32 [384, 384], P('fsdp')
- b_out: float32 [384], P('fsdp')
- ln2_g: float32 [384], P('fsdp')
- ln2_b: float32 [384], P('fsdp')
- w_fc: float32 [384, 1536], P('fsdp')
- b_fc: float32 [1536], P('fsdp')
- w_proj: float32 [1536, 384], P('fsdp')
- b_proj: float32 [384], P('fsdp')
- grad_h1: bfloat16 [64, 99, 384], P('fsdp')
Outputs:
- output 1: bfloat16 [64, 99, 384], P('fsdp')
- output 2: float32 [768, 384], P(None, 'fsdp')
- output 3: float32 [384], P('fsdp')
- output 4: float32 [197, 384], P(None, 'fsdp')
- output 5: float32 [384], P('fsdp')
- output 6: float32 [384], P('fsdp')
- output 7: float32 [384], P('fsdp')
- output 8: float32 [384], P('fsdp')
- output 9: float32 [384], P('fsdp')
- output 10: float32 [384, 3, 6, 64], P('fsdp')
- output 11: float32 [1152], P('fsdp')
- output 12: float32 [384, 384], P('fsdp')
- output 13: float32 [384], P('fsdp')
- output 14: float32 [384], P('fsdp')
- output 15: float32 [384], P('fsdp')
- output 16: float32 [384, 1536], P('fsdp')
- output 17: float32 [1536], P('fsdp')
- output 18: float32 [1536, 384], P('fsdp')
- output 19: float32 [384], P('fsdp')
All inputs are finite; a program needn't handle non-finite values.
Results may differ from a plain program's by a relative error of at most 0.02.
Values are sent between devices in bfloat16 or wider.
A program may use at most 1 GiB of HBM per device.

v0:
```python
import jax
import jax.numpy as jnp
from jax import lax
from jax.sharding import PartitionSpec as P

MESH_AXIS = 'fsdp'
LN_EPS = 1e-5
INV_SQRT2 = 0.7071067811865476
INV_SQRT_2PI = 0.3989422804014327
PARAM_NAMES = ('w_patch', 'b_patch', 'pos_table', 'cls_tok', 'lnp_g', 'lnp_b', 'ln1_g', 'ln1_b', 'w_qkv', 'b_qkv', 'w_out', 'b_out', 'ln2_g', 'ln2_b', 'w_fc', 'b_fc', 'w_proj', 'b_proj')
VECTOR_NAMES = ('b_patch', 'cls_tok', 'lnp_g', 'lnp_b', 'ln1_g', 'ln1_b', 'b_qkv', 'b_out', 'ln2_g', 'ln2_b', 'b_fc', 'b_proj')
BACKWARD_NAMES = ('w_qkv', 'w_out', 'w_fc', 'w_proj', 'lnp_g', 'ln1_g', 'ln2_g')
LAST_SPLIT = ('w_patch', 'pos_table')


def product(einsum_form, left_op, right_op):
    return jnp.einsum(einsum_form, left_op, right_op, preferred_element_type=jnp.float32)


def norm_forward(x_in, gain_f, shift_f):
    centered = x_in - jnp.mean(x_in, axis=-1, keepdims=True)
    inv_std = lax.rsqrt(jnp.mean(centered * centered, axis=-1, keepdims=True) + LN_EPS)
    x_hat = centered * inv_std
    return x_hat * gain_f + shift_f, x_hat, inv_std


def norm_backward(d_norm, x_hat, inv_std, gain_f):
    d_hat = d_norm * gain_f
    d_in = inv_std * (d_hat - jnp.mean(d_hat, axis=-1, keepdims=True) - x_hat * jnp.mean(d_hat * x_hat, axis=-1, keepdims=True))
    return d_in, jnp.sum(d_norm * x_hat, axis=(0, 1)), jnp.sum(d_norm, axis=(0, 1))


def gelu_slope(pre_act):
    return 0.5 * (1.0 + lax.erf(pre_act * INV_SQRT2)) + pre_act * jnp.exp(-0.5 * pre_act * pre_act) * INV_SQRT_2PI


def forward(full_w, patches, keep):
    n_img, n_patch = patches.shape[0], patches.shape[1]
    d_model = full_w['w_out'].shape[0]
    n_heads, head_dim = full_w['w_qkv'].shape[2], full_w['w_qkv'].shape[3]
    logit_scale = head_dim ** -0.5
    as_f32 = {name: full_w[name].astype(jnp.float32) for name in VECTOR_NAMES}
    onehot_keep = (keep[:, :, None] == lax.broadcasted_iota(jnp.int32, (1, 1, n_patch), 2)).astype(jnp.bfloat16)
    kept_rows = product('bkp,bpq->bkq', onehot_keep, patches).astype(jnp.bfloat16)
    embed_rows = (product('bkq,qw->bkw', kept_rows, full_w['w_patch']) + as_f32['b_patch']
                  + product('bkp,pw->bkw', onehot_keep, full_w['pos_table'][1:]))
    head_row = as_f32['cls_tok'] + full_w['pos_table'][0].astype(jnp.float32)
    x_zero = jnp.concatenate([jnp.broadcast_to(head_row, (n_img, 1, d_model)), embed_rows], axis=1)
    h_zero, hat_p, inv_p = norm_forward(x_zero, as_f32['lnp_g'], as_f32['lnp_b'])
    y_one, hat_1, inv_1 = norm_forward(h_zero, as_f32['ln1_g'], as_f32['ln1_b'])
    a_in = y_one.astype(jnp.bfloat16)
    qkv_all = (product('btw,wchd->btchd', a_in, full_w['w_qkv']) + as_f32['b_qkv'].reshape(3, n_heads, head_dim)).astype(jnp.bfloat16)
    q_heads, k_heads, v_heads = qkv_all[:, :, 0], qkv_all[:, :, 1], qkv_all[:, :, 2]
    attn_prob = jax.nn.softmax(product('bqhd,bkhd->bhqk', q_heads, k_heads) * logit_scale, axis=-1)
    prob_b = attn_prob.astype(jnp.bfloat16)
    context = product('bhqk,bkhd->bqhd', prob_b, v_heads).astype(jnp.bfloat16)
    h_mid = h_zero + product('bqhd,hdw->bqw', context, full_w['w_out'].reshape(n_heads, head_dim, d_model)) + as_f32['b_out']
    y_two, hat_2, inv_2 = norm_forward(h_mid, as_f32['ln2_g'], as_f32['ln2_b'])
    c_in = y_two.astype(jnp.bfloat16)
    pre_act = product('btw,wf->btf', c_in, full_w['w_fc']) + as_f32['b_fc']
    gelu_out = jax.nn.gelu(pre_act, approximate=False).astype(jnp.bfloat16)
    h_one = (h_mid + product('btf,fw->btw', gelu_out, full_w['w_proj']) + as_f32['b_proj']).astype(jnp.bfloat16)
    saved = dict(onehot_keep=onehot_keep, kept_rows=kept_rows, hat_p=hat_p, inv_p=inv_p, hat_1=hat_1, inv_1=inv_1, a_in=a_in, q_heads=q_heads, k_heads=k_heads, v_heads=v_heads, attn_prob=attn_prob, prob_b=prob_b, context=context, hat_2=hat_2, inv_2=inv_2, c_in=c_in, pre_act=pre_act, gelu_out=gelu_out)
    return h_one, saved


def backward(weights, saved, grad_h1):
    d_model = weights['w_out'].shape[0]
    n_heads, head_dim = weights['w_qkv'].shape[2], weights['w_qkv'].shape[3]
    logit_scale = head_dim ** -0.5
    w_out3 = weights['w_out'].reshape(n_heads, head_dim, d_model)
    d_h = grad_h1.astype(jnp.float32)
    g_w_proj = product('btf,btw->fw', saved['gelu_out'], grad_h1)
    d_pre = product('btw,fw->btf', grad_h1, weights['w_proj']) * gelu_slope(saved['pre_act'])
    d_pre_b = d_pre.astype(jnp.bfloat16)
    g_w_fc = product('btw,btf->wf', saved['c_in'], d_pre_b)
    d_c = product('btf,wf->btw', d_pre_b, weights['w_fc'])
    d_norm2, g_ln2_g, g_ln2_b = norm_backward(d_c, saved['hat_2'], saved['inv_2'], weights['ln2_g'].astype(jnp.float32))
    d_mid = d_norm2 + d_h
    d_mid_b = d_mid.astype(jnp.bfloat16)
    g_w_out = product('bqhd,bqw->hdw', saved['context'], d_mid_b).reshape(d_model, d_model)
    d_ctx = product('bqw,hdw->bqhd', d_mid_b, w_out3).astype(jnp.bfloat16)
    g_v = product('bhqk,bqhd->bkhd', saved['prob_b'], d_ctx)
    d_prob = product('bqhd,bkhd->bhqk', d_ctx, saved['v_heads'])
    attn_prob = saved['attn_prob']
    d_logit = (attn_prob * (d_prob - jnp.sum(attn_prob * d_prob, axis=-1, keepdims=True)) * logit_scale).astype(jnp.bfloat16)
    g_q = product('bhqk,bkhd->bqhd', d_logit, saved['k_heads'])
    g_k = product('bhqk,bqhd->bkhd', d_logit, saved['q_heads'])
    d_qkv = jnp.stack([g_q, g_k, g_v], axis=2)
    d_qkv_b = d_qkv.astype(jnp.bfloat16)
    g_w_qkv = product('btw,btchd->wchd', saved['a_in'], d_qkv_b)
    d_a = product('btchd,wchd->btw', d_qkv_b, weights['w_qkv'])
    d_norm1, g_ln1_g, g_ln1_b = norm_backward(d_a, saved['hat_1'], saved['inv_1'], weights['ln1_g'].astype(jnp.float32))
    d_zero = d_norm1 + d_mid
    d_x, g_lnp_g, g_lnp_b = norm_backward(d_zero, saved['hat_p'], saved['inv_p'], weights['lnp_g'].astype(jnp.float32))
    d_head = jnp.sum(d_x[:, 0], axis=0)
    d_emb = d_x[:, 1:]
    d_emb_b = d_emb.astype(jnp.bfloat16)
    g_pos = jnp.concatenate([d_head[None], product('bkp,bkw->pw', saved['onehot_keep'], d_emb_b)], axis=0)
    return dict(w_patch=product('bkq,bkw->qw', saved['kept_rows'], d_emb_b), b_patch=jnp.sum(d_emb, axis=(0, 1)), pos_table=g_pos, cls_tok=d_head, lnp_g=g_lnp_g, lnp_b=g_lnp_b, ln1_g=g_ln1_g, ln1_b=g_ln1_b, w_qkv=g_w_qkv, b_qkv=jnp.sum(d_qkv, axis=(0, 1)).reshape(-1), w_out=g_w_out, b_out=jnp.sum(d_mid, axis=(0, 1)), ln2_g=g_ln2_g, ln2_b=g_ln2_b, w_fc=g_w_fc, b_fc=jnp.sum(d_pre, axis=(0, 1)), w_proj=g_w_proj, b_proj=jnp.sum(d_h, axis=(0, 1)))


def solution(mesh):
    def split_of(name):
        return 1 if name in LAST_SPLIT else 0

    def spec_of(name):
        return P(None, MESH_AXIS) if name in LAST_SPLIT else P(MESH_AXIS)

    def gather_whole(shard, name):
        return lax.all_gather(shard.astype(jnp.bfloat16), MESH_AXIS, axis=split_of(name), tiled=True)

    def local_step(patches, keep, *rest):
        shards = dict(zip(PARAM_NAMES, rest[:-1]))
        grad_h1 = rest[-1]
        full_w = {name: gather_whole(shards[name], name) for name in PARAM_NAMES}
        h_one, saved = forward(full_w, patches, keep)
        held, h_one = lax.optimization_barrier((shards, h_one))
        regathered = {name: gather_whole(held[name], name) for name in BACKWARD_NAMES}
        grad_map = backward(regathered, saved, grad_h1)
        summed = tuple(lax.psum_scatter(grad_map[name], MESH_AXIS, scatter_dimension=split_of(name), tiled=True) for name in PARAM_NAMES)
        return (h_one,) + summed

    batch_spec = P(MESH_AXIS)
    param_specs = tuple(spec_of(name) for name in PARAM_NAMES)
    return jax.shard_map(local_step, mesh=mesh, in_specs=(batch_spec, batch_spec) + param_specs + (batch_spec,), out_specs=(batch_spec,) + param_specs, check_vma=False)
```

profile of v0, /device:TPU:0, one launch (start us, length us, event | category | flops | bytes accessed | tf_op | source)
XLA Modules:
  0.0 455.2 jit_solution(15155674759558553775)
XLA Ops:
  21.4 25.5 %all-reduce.29 = (bf16[1152]{0:T(1024)(128)(2,1)S(1)}, bf16[384]{0:T(512)(128)(2,1)S(1)}, bf16[384]{0:T(512)(128)(2,1)S(1)}, bf16[384]{0:T(512)(128)(2,1)S(1)}, ...) all-reduce(bf16[1152]{0:T(1024)(128)(2,1)S(1)} %dynamic-update-slic, ...), channel_id=1, replica_groups=mesh['fsdp'=8] {'fsdp'}, use_global_device_ids=true, to_apply=%add.6 | all-reduce | flops 6528 | bytes 26112
  48.9 12.2 %all_gather.76 = bf16[197,384]{0,1:T(8,128)(2,1)S(1)} all-gather(bf16[197,48]{0,1:T(8,128)(2,1)S(1)} %convert_element_type.175), channel_id=1, replica_groups=mesh['fsdp'=8] {'fsdp'}, dimensions={1}, use_global_device_ids=true | all-gather | bytes 170208 | tf_op jit(solution)/shard_map/all_gather | solution.py:111
  61.2 11.6 %all_gather.85 = bf16[384,384]{1,0:T(8,128)(2,1)S(1)} all-gather(bf16[48,384]{1,0:T(8,128)(2,1)S(1)} %convert_element_type.197), channel_id=1, replica_groups=mesh['fsdp'=8] {'fsdp'}, dimensions={0}, use_global_device_ids=true | all-gather | bytes 331776 | tf_op jit(solution)/shard_map/all_gather | solution.py:111
  72.8 12.5 %all_gather.77 = bf16[768,384]{0,1:T(8,128)(2,1)S(1)} all-gather(bf16[768,48]{0,1:T(8,128)(2,1)S(1)} %convert_element_type.179), channel_id=1, replica_groups=mesh['fsdp'=8] {'fsdp'}, dimensions={1}, use_global_device_ids=true | all-gather | bytes 663552 | tf_op jit(solution)/shard_map/all_gather | solution.py:111
  90.3 18.0 %all_gather.83 = bf16[384,3,6,64]{3,0,2,1:T(8,128)(2,1)S(1)} all-gather(bf16[48,3,6,64]{3,0,2,1:T(8,128)(2,1)S(1)} %convert_element_type.191), channel_id=1, replica_groups=mesh['fsdp'=8] {'fsdp'}, dimensions={0}, use_global_device_ids=true | all-gather | bytes 995328 | tf_op jit(solution)/shard_map/all_gather | solution.py:111
  108.3 2.7 add_convert_fusion
  111.9 2.9 fusion.92
  118.6 4.7 %fusion.59 = (u8[99,1536]{1,0:T(8,128)(4,1)S(1)}, u8[99,1536]{1,0:T(8,128)(4,1)S(1)}, f32[8,99,1536]{2,1,0:T(8,128)S(1)}) fusion(f32[1536]{0:T(1024)S(1)} %convert_element_type.207, bf16[384,1536]{1,0:T(8,128)(2,1)} %all-gather.5.cloned.1.call-done, f32[8,99,384]{2,1,0:T(8,128)} %copy-done.5, f32[384]{0:T(512)S(1)} %convert_element_type.203, ...), kind=kOutput, calls=%fused_computation.92 | convolution fusion | flops 952528896 | bytes 7581888 | tf_op jit(solution)/shard_map/btw,wf->btf/dot_general | solution.py:17
  123.4 2.2 copy-done.9
  125.6 12.5 %fusion.4 = bf16[8,99,1536]{2,1,0:T(8,128)(2,1)} fusion(f32[8,99,1536]{2,1,0:T(8,128)S(1)} %get-tuple-element.141, f32[1536]{0:T(1024)S(1)} %convert_element_type.207, u8[99,1536]{1,0:T(8,128)(4,1)S(1)} %get-tuple-element.93, u8[99,1536]{1,0:T(8,128)(4,1)S(1)} %get-tuple-element.92), kind=kLoop, calls=%fused_computation.6 | loop fusion | flops 86372352 | bytes 7609344 | tf_op jit(solution)/shard_map/convert_element_type | solution.py:61
  138.2 4.9 %fusion.50 = bf16[8,99,384]{2,1,0:T(8,128)(2,1)} fusion(f32[8,99,384]{2,1,0:T(8,128)} %copy-done.5, bf16[8,99,1536]{2,1,0:T(8,128)(2,1)} %fusion.4, bf16[1536,384]{1,0:T(8,128)(2,1)} %all-gather.7.cloned.1.call-done, f32[384]{0:T(512)S(1)} %convert_element_type.211), kind=kOutput, calls=%fused_computation.67 | convolution fusion | flops 935193600 | bytes 5438976 | tf_op jit(solution)/shard_map/btf,fw->btw/dot_general | solution.py:17
  145.3 22.4 %all-reduce.28 = (bf16[384]{0:T(512)(128)(2,1)S(1)}, bf16[384]{0:T(512)(128)(2,1)S(1)}, bf16[384]{0:T(512)(128)(2,1)S(1)}) all-reduce(bf16[384]{0:T(512)(128)(2,1)S(1)} %dynamic-update-slice.12, bf16[384]{0:T(512)(128)(2,1)S(1)} %dynamic-update-slice.13, bf16[384]{0:T(512)(128)(2,1)S(1)} %dynamic-update-slice.14), channel_id=1, replica_groups=mesh['fsdp'=8] {'fsdp'}, use_global_device_ids=true, to_apply=%add.12 | all-reduce | flops 1152 | bytes 4608
  167.8 13.2 %all_gather.96 = bf16[384,384]{1,0:T(8,128)(2,1)S(1)} all-gather(bf16[48,384]{1,0:T(8,128)(2,1)S(1)} %convert_element_type.220), channel_id=1, replica_groups=mesh['fsdp'=8] {'fsdp'}, dimensions={0}, use_global_device_ids=true | all-gather | bytes 331776 | tf_op jit(solution)/shard_map/all_gather | solution.py:111
  181.0 17.7 %all_gather.97 = bf16[384,3,6,64]{3,0,2,1:T(8,128)(2,1)} all-gather(bf16[48,3,6,64]{3,0,2,1:T(8,128)(2,1)S(1)} %convert_element_type.224), channel_id=1, replica_groups=mesh['fsdp'=8] {'fsdp'}, dimensions={0}, use_global_device_ids=true | all-gather | bytes 995328 | tf_op jit(solution)/shard_map/all_gather | solution.py:111
  198.8 7.0 %fusion.94 = (f32[1536]{0:T(1024)}, bf16[8,99,1536]{2,1,0:T(8,128)(2,1)}) fusion(f32[8,99,1536]{2,1,0:T(8,128)} %copy-done.9, f32[1536]{0:T(1024)S(1)} %convert_element_type.207, bf16[8,99,384]{2,0,1:T(8,128)(2,1)S(1)} %copy-done.19, bf16[1536,384]{1,0:T(8,128)(2,1)} %all-gather.9.cloned.1.call-done), kind=kOutput, calls=%fused_computation.155 | convolution fusion | flops 948877824 | bytes 9099264 | tf_op jit(solution)/shard_map/btw,fw->btf/dot_general | solution.py:17
  205.7 4.9 %multiply_reduce_fusion.2 = (f32[384]{0:T(512)}, f32[8,99]{1,0:T(8,128)S(1)}, f32[8,99]{1,0:T(8,128)S(1)}, f32[384]{0:T(512)}, f32[8,99,384]{2,1,0:T(8,128)S(1)}) fusion(f32[8,99,384]{2,1,0:T(8,128)} %copy-done.5, f32[8,99]{1,0:T(8,128)S(1)} %add_rsqrt_fusion, f32[8,99]{1,0:T(8,128)S(1)} %broadcast_multiply_fusion.6, f32[384]{0:T(512)S(1)} %convert_element_type.217, ...), kind=kOutput, calls=%fused_computation.70 | convolution fusion | flops 937016064 | bytes 6062976 | tf_op jit(solution)/shard_map/btf,wf->btw/dot_general | solution.py:17
  212.6 2.1 convolution_bitcast_fusion.3
  214.8 3.5 fusion.65
  218.2 6.4 %fusion.38 = f32[8,99,1,6,64]{1,4,3,0,2:T(8,128)} fusion(f32[8,6,99,99]{2,3,1,0:T(8,128)} %fusion.65, bf16[8,99,3,6,64]{1,4,3,2,0:T(8,128)(2,1)} %copy-done.12, f32[8,6,99,99]{2,3,1,0:T(8,128)} %copy-done.10, f32[8,6,99]{2,1,0:T(8,128)S(1)} %get-tuple-element.137), kind=kOutput, calls=%fused_computation.53 | convolution fusion | flops 63515328 | bytes 12292096 | tf_op jit(solution)/shard_map/bhqk,bkhd->bqhd/dot_general | solution.py:17
  224.7 6.4 %fusion.41 = f32[8,99,1,6,64]{1,4,3,0,2:T(8,128)} fusion(f32[8,6,99,99]{2,3,1,0:T(8,128)} %fusion.65, bf16[8,99,3,6,64]{1,4,3,2,0:T(8,128)(2,1)} %copy-done.12, f32[8,6,99,99]{2,3,1,0:T(8,128)} %copy-done.10, f32[8,6,99]{2,1,0:T(8,128)S(1)} %get-tuple-element.137), kind=kOutput, calls=%fused_computation.54 | convolution fusion | flops 63515328 | bytes 12292096 | tf_op jit(solution)/shard_map/bhqk,bqhd->bkhd/dot_general | solution.py:17
  231.0 6.3 %multiply_reduce_fusion.3 = (f32[384]{0:T(512)S(1)}, f32[8,99]{1,0:T(8,128)S(1)}, f32[8,99]{1,0:T(8,128)S(1)}, f32[384]{0:T(512)S(1)}, f32[8,99,384]{2,1,0:T(8,128)S(1)}) fusion(f32[8,99]{1,0:T(8,128)S(1)} %add_rsqrt_fusion.1, f32[8,99]{1,0:T(8,128)S(1)} %broadcast_multiply_fusion.7, f32[384]{0:T(512)S(1)} %convert_element_type.185, ...), kind=kOutput, calls=%fused_computation.71 | convolution fusion | flops 706791168 | bytes 6993984 | tf_op jit(solution)/shard_map/btchd,wchd->btw/dot_general | solution.py:17
  242.2 2.8 fusion.69
  245.3 4.8 %convolution_bitcast_fusion = f32[1536,384]{1,0:T(8,128)} fusion(bf16[8,99,1536]{2,1,0:T(8,128)(2,1)} %fusion.4, bf16[8,99,384]{2,0,1:T(8,128)(2,1)S(1)} %copy-done.20), kind=kOutput, calls=%fused_computation.34 | convolution fusion | flops 934281216 | bytes 5400576 | tf_op jit(solution)/shard_map/btf,btw->fw/dot_general | solution.py:17
  250.3 3.5 convolution_bitcast_fusion.5
  253.9 6.8 %convolution_bitcast_fusion.2 = f32[384,3,6,64]{3,0,2,1:T(8,128)} fusion(f32[384]{0:T(512)S(1)} %copy-done.30, f32[384]{0:T(512)S(1)} %copy-done.32, f32[8,99]{1,0:T(8,128)S(1)} %add_rsqrt_fusion.1, f32[8,99]{1,0:T(8,128)S(1)} %broadcast_multiply_fusion.7, f32[8,99,1,6,64]{1,4,3,0,2:T(8,128)} %convolution_bitcast_fusion.3, ...), kind=kOutput, calls=%fused_computation.44 | convolution fusion | flops 709226496 | bytes 6654336 | tf_op jit(solution)/shard_map/btw,btchd->wchd/dot_general | solution.py:17
  262.0 4.7 %convolution_bitcast_fusion.1 = f32[384,1536]{1,0:T(8,128)} fusion(bf16[8,99,1536]{2,1,0:T(8,128)(2,1)} %get-tuple-element.145, f32[8,99,384]{2,1,0:T(8,128)S(1)} %copy-done.7, f32[384]{0:T(512)S(1)} %convert_element_type.203, f32[384]{0:T(512)S(1)} %convert_element_type.201, f32[8,99]{1,0:T(8,128)S(1)} %add_rsqrt_fusion, ...), kind=kOutput, calls=%fused_computation.35 | convolution fusion | flops 935801856 | bytes 6018240 | tf_op jit(solution)/shard_map/btw,btf->wf/dot_general | solution.py:17
  268.7 3.0 fusion.16
  273.4 22.9 %all-reduce.27 = (f32[384]{0:T(512)S(1)}, f32[384]{0:T(512)S(1)}, f32[384]{0:T(512)S(1)}, f32[384]{0:T(512)S(1)}, f32[384]{0:T(512)S(1)}, /*index=5*/f32[384]{0:...) all-reduce(f32[384]{0:T(512)S(1)} %slice_reduce_fusion, ...), channel_id=3, replica_groups=mesh['fsdp'=8] {'fsdp'}, use_global_device_ids=true, to_apply=%region_17.0.clone | all-reduce | flops 6528 | bytes 52224
  303.4 31.6 %reduce-scatter.17.cloned.1.call-done = f32[192,384]{1,0:T(8,128)} async-done(((f32[1536,384]{1,0:T(8,128)}), f32[192,384]{1,0:T(8,128)}) %reduce-scatter.17.cloned.1.call-update) | async-done | bytes 294928 | tf_op jit(solution)/shard_map/reduce_scatter | solution.py:121
  335.0 32.0 %reduce-scatter.9.cloned.1.call-done = f32[768,48]{0,1:T(8,128)} async-done(((f32[768,384]{0,1:T(8,128)}), f32[768,48]{0,1:T(8,128)}) %reduce-scatter.9.cloned.1.call-update) | async-done | bytes 147472 | tf_op jit(solution)/shard_map/reduce_scatter | solution.py:121
  367.0 43.4 %reduce-scatter.11.cloned.1.call-done = f32[48,3,6,64]{3,0,2,1:T(8,128)} async-done(((f32[384,3,6,64]{3,0,2,1:T(8,128)}), f32[48,3,6,64]{3,0,2,1:T(8,128)}) %reduce-scatter.11.cloned.1.call-update) | async-done | bytes 221200 | tf_op jit(solution)/shard_map/reduce_scatter | solution.py:121
  410.4 37.6 %reduce-scatter.15.cloned.1.call-done = f32[48,1536]{1,0:T(8,128)} async-done(((f32[384,1536]{1,0:T(8,128)}), f32[48,1536]{1,0:T(8,128)}) %reduce-scatter.15.cloned.1.call-update) | async-done | bytes 294928 | tf_op jit(solution)/shard_map/reduce_scatter | solution.py:121
  (215 shorter events, 47.2 us)
Async XLA Ops:
  7.2 78.1 %copy-start = (bf16[8,196,768]{2,0,1:T(8,128)(2,1)S(1)}, bf16[8,196,768]{2,0,1:T(8,128)(2,1)}, u32[]{:S(2)}) copy-start(bf16[8,196,768]{2,0,1:T(8,128)(2,1)} %param.21) | copy-start | bytes 7225348
  7.2 41.6 %copy-start.22 = (f32[768,48]{0,1:T(8,128)S(1)}, f32[768,48]{0,1:T(8,128)}, u32[]{:S(2)}) copy-start(f32[768,48]{0,1:T(8,128)} %param.23) | copy-start | bytes 442372
  7.2 54.0 %copy-start.13 = (f32[48,3,6,64]{3,0,2,1:T(8,128)S(1)}, f32[48,3,6,64]{3,0,2,1:T(8,128)}, u32[]{:S(2)}) copy-start(f32[48,3,6,64]{3,0,2,1:T(8,128)} %param.31) | copy-start | bytes 663556
  7.2 111.4 %all-gather.5.cloned.1.call-start = ((), (), s32[]{:S(2)}) async-start(), calls=%async_computation.6 | async-start | bytes 1327104 | tf_op jit(solution)/shard_map/all_gather | solution.py:111
  9.1 76.2 %copy-start.23 = (s32[8,98]{1,0:T(8,128)S(1)}, s32[8,98]{1,0:T(8,128)}, u32[]{:S(2)}) copy-start(s32[8,98]{1,0:T(8,128)} %param.22) | copy-start | bytes 9412
  9.1 129.1 %all-gather.7.cloned.1.call-start = ((), (), s32[]{:S(2)}) async-start(), calls=%async_computation.7 | async-start | bytes 1327104 | tf_op jit(solution)/shard_map/all_gather | solution.py:111
  10.8 187.9 %all-gather.9.cloned.1.call-start = ((), (), s32[]{:S(2)}) async-start(), calls=%async_computation.8 | async-start | bytes 1327104 | tf_op jit(solution)/shard_map/all_gather | solution.py:111
  47.0 61.4 %copy-start.29 = (f32[384]{0:T(512)}, f32[384]{0:T(512)S(1)}, u32[]{:S(2)}) copy-start(f32[384]{0:T(512)S(1)} %convert_element_type.189) | copy-start | bytes 4612
  47.0 61.3 %copy-start.31 = (f32[384]{0:T(512)}, f32[384]{0:T(512)S(1)}, u32[]{:S(2)}) copy-start(f32[384]{0:T(512)S(1)} %convert_element_type.187) | copy-start | bytes 4612
  111.0 3.8 copy-start.12
  138.1 5.0 %copy-start.14 = (f32[192,384]{1,0:T(8,128)S(1)}, f32[192,384]{1,0:T(8,128)}, u32[]{:S(2)}) copy-start(f32[192,384]{1,0:T(8,128)} %param.39) | copy-start | bytes 884740
  138.1 5.7 %copy-start.15 = (f32[48,1536]{1,0:T(8,128)S(1)}, f32[48,1536]{1,0:T(8,128)}, u32[]{:S(2)}) copy-start(f32[48,1536]{1,0:T(8,128)} %param.37) | copy-start | bytes 884740
  138.1 6.5 %copy-start.33 = (f32[48]{0:T(128)S(1)}, f32[48]{0:T(128)}, u32[]{:S(2)}) copy-start(f32[48]{0:T(128)} %param.35) | copy-start | bytes 580
  138.1 6.5 %copy-start.34 = (f32[48]{0:T(128)S(1)}, f32[48]{0:T(128)}, u32[]{:S(2)}) copy-start(f32[48]{0:T(128)} %param.29) | copy-start | bytes 580
  138.1 6.5 %copy-start.35 = (f32[48]{0:T(128)S(1)}, f32[48]{0:T(128)}, u32[]{:S(2)}) copy-start(f32[48]{0:T(128)} %param.27) | copy-start | bytes 580
  138.1 29.7 %copy-start.21 = (f32[48,384]{1,0:T(8,128)S(1)}, f32[48,384]{1,0:T(8,128)}, u32[]{:S(2)}) copy-start(f32[48,384]{1,0:T(8,128)} %param.33) | copy-start | bytes 221188
  143.8 62.0 %all-gather.11.cloned.1.call-start = ((), (), s32[]{:S(2)}) async-start(), calls=%async_computation.9 | async-start | bytes 1327104 | tf_op jit(solution)/shard_map/all_gather | solution.py:111
  144.5 54.2 %copy-start.19 = (bf16[8,99,384]{2,0,1:T(8,128)(2,1)S(1)}, bf16[8,99,384]{2,0,1:T(8,128)(2,1)}, u32[]{:S(2)}) copy-start(bf16[8,99,384]{2,0,1:T(8,128)(2,1)} %param.41) | copy-start | bytes 1824772
  144.5 158.9 %reduce-scatter.19.cloned.1.call-start = ((), (), s32[]{:S(2)}) async-start(), calls=%async_computation.15 | async-start | bytes 442368
  205.7 4.9 %copy-start.6 = (f32[8,99,384]{2,1,0:T(8,128)S(1)}, f32[8,99,384]{2,1,0:T(8,128)}, u32[]{:S(2)}) copy-start(f32[8,99,384]{2,1,0:T(8,128)} %copy-done.5) | copy-start | bytes 3649540
  231.0 6.3 %copy-start.4 = (f32[8,99,384]{2,1,0:T(8,128)S(1)}, f32[8,99,384]{2,1,0:T(8,128)}, u32[]{:S(2)}) copy-start(f32[8,99,384]{2,1,0:T(8,128)} %copy-done.3) | copy-start | bytes 3649540
  242.2 61.2 %reduce-scatter.13.cloned.1.call-start = ((), (), s32[]{:S(2)}) async-start(), calls=%async_computation.12 | async-start | bytes 663552 | tf_op jit(solution)/shard_map/reduce_scatter | solution.py:121
  245.0 90.0 %reduce-scatter.17.cloned.1.call-start = ((), (), s32[]{:S(2)}) async-start(), calls=%async_computation.14 | async-start | bytes 2654208 | tf_op jit(solution)/shard_map/reduce_scatter | solution.py:121
  250.2 116.8 %reduce-scatter.9.cloned.1.call-start = ((), (), s32[]{:S(2)}) async-start(), calls=%async_computation.10 | async-start | bytes 1327104 | tf_op jit(solution)/shard_map/reduce_scatter | solution.py:121
  253.8 156.5 %reduce-scatter.11.cloned.1.call-start = ((), (), s32[]{:S(2)}) async-start(), calls=%async_computation.11 | async-start | bytes 3981312 | tf_op jit(solution)/shard_map/reduce_scatter | solution.py:121
  260.7 187.2 %reduce-scatter.15.cloned.1.call-start = ((), (), s32[]{:S(2)}) async-start(), calls=%async_computation.13 | async-start | bytes 2654208 | tf_op jit(solution)/shard_map/reduce_scatter | solution.py:121
  268.7 4.7 %copy-start.24 = (f32[384]{0:T(512)S(1)}, f32[384]{0:T(512)}, u32[]{:S(2)}) copy-start(f32[384]{0:T(512)} %get-tuple-element.133) | copy-start | bytes 4612
  268.7 4.7 %copy-start.25 = (f32[384]{0:T(512)S(1)}, f32[384]{0:T(512)}, u32[]{:S(2)}) copy-start(f32[384]{0:T(512)} %get-tuple-element.136) | copy-start | bytes 4612
  268.7 4.7 %copy-start.26 = (f32[1536]{0:T(1024)S(1)}, f32[1536]{0:T(1024)}, u32[]{:S(2)}) copy-start(f32[1536]{0:T(1024)} %get-tuple-element.144) | copy-start | bytes 18436
  268.7 4.7 %copy-start.27 = (f32[384]{0:T(512)S(1)}, f32[384]{0:T(512)}, u32[]{:S(2)}) copy-start(f32[384]{0:T(512)} %get-tuple-element.98) | copy-start | bytes 4612
  268.7 4.7 %copy-start.28 = (f32[384]{0:T(512)S(1)}, f32[384]{0:T(512)}, u32[]{:S(2)}) copy-start(f32[384]{0:T(512)} %get-tuple-element.103) | copy-start | bytes 4612
  268.7 179.2 %copy-start.1 = (bf16[8,196,768]{2,0,1:T(8,128)(2,1)S(1)}, bf16[8,196,768]{2,0,1:T(8,128)(2,1)}, u32[]{:S(2)}) copy-start(bf16[8,196,768]{2,0,1:T(8,128)(2,1)} %param.21) | copy-start | bytes 7225348
  (14 other events, 27.1 us)
Sparse Core Ops, SparseCore 0:
  10.4 21.3 all-gather.4
  34.2 18.2 all-gather.6
  143.9 18.3 all-gather.8
  164.5 18.9 all-gather.10
  242.3 25.5 reduce-scatter.18
  271.3 26.0 reduce-scatter.12
  301.2 33.7 reduce-scatter.16
  338.7 28.2 reduce-scatter.8
  371.0 39.3 reduce-scatter.10
  414.1 33.8 reduce-scatter.14
where the time goes:
time: 463 us; the launch traced here: 455 us
  blocking collectives  156 us (34%)
  waiting for transfers between devices  145 us (31%)
  matrix products  77.6 us (17%)
  other arithmetic  40.5 us (9%)
  local copies, waits for them, and re-layouts  20.4 us (4%)
  between operations  15.4 us (3%)
    reduce_scatter x5, waiting for transfers between devices, local_step(): lax.psum_scatter(grad_map[name], MESH_AXIS, scatter_dimension=split_of(na...  145 us
    all_gather x6, blocking collectives, gather_whole(): lax.all_gather(shard.astype(jnp.bfloat16), MESH_AXIS, axis=split_of(name)...  85.1 us
    dot_general x23, matrix products, product(): jnp.einsum(einsum_form, left_op, right_op, preferred_element_type=jnp.flo...  77.6 us
    unnamed x3, blocking collectives  70.9 us
    unnamed x116, local copies, waits for them, and re-layouts  20.2 us
    convert_element_type x25, other arithmetic, gather_whole(): shard.astype(jnp.bfloat16)  14.5 us
    convert_element_type x1, other arithmetic, forward(): gelu_out = jax.nn.gelu(pre_act, approximate=False).astype(jnp.bfloat16)  12.5 us
  transfers between devices with their start and end apart: 10, of which 4 were waited for; matrix products, arithmetic and copies ran while one was open for 19% of the time, Pallas kernels for 0%

commit v1 on v0

v1 whole, which is shorter than its diff:
```python
import functools

import jax
import jax.numpy as jnp
from jax import lax
from jax.experimental import pallas as pl
from jax.experimental.pallas import tpu as pltpu
from jax.sharding import PartitionSpec as P

AXIS = 'fsdp'
LN_EPS = 1e-5
INV_SQRT2 = 0.7071067811865476
INV_SQRT_2PI = 0.3989422804014327
PARAM_NAMES = ('w_patch', 'b_patch', 'pos_table', 'cls_tok', 'lnp_g', 'lnp_b', 'ln1_g', 'ln1_b', 'w_qkv', 'b_qkv', 'w_out', 'b_out', 'ln2_g', 'ln2_b', 'w_fc', 'b_fc', 'w_proj', 'b_proj')
VROWS = ('b_patch', 'cls_tok', 'lnp_g', 'lnp_b', 'ln1_g', 'ln1_b', 'b_out', 'ln2_g', 'ln2_b', 'b_proj', 'b_qkv', 'b_fc')
ROW = {name: i for i, name in enumerate(VROWS)}
LAST_SPLIT = ('w_patch', 'pos_table')
MESH = pl.DeviceIdType.MESH

NDEV = 8
IMG = 8
NPATCH = 196
NKEEP = 98
TOK = 99
TP = 112
NT = IMG * TP
D = 384
HD = 64
PAIRS = 3
FF = 1536
QKV3 = 1152
PX = 768
PPOS = 256
SUB = D // NDEV
SUBF = FF // NDEV
RB = 224
F32 = jnp.float32
BF16 = jnp.bfloat16


def dot(a, b):
    return jnp.dot(a, b, preferred_element_type=F32)


def dot_nt(a, b):
    return lax.dot_general(a, b, (((1,), (1,)), ((), ())), preferred_element_type=F32)


def dot_tn(a, b):
    return lax.dot_general(a, b, (((0,), (0,)), ((), ())), preferred_element_type=F32)


def norm_stats(x):
    mu = jnp.mean(x, axis=-1, keepdims=True)
    c = x - mu
    inv = lax.rsqrt(jnp.mean(c * c, axis=-1, keepdims=True) + LN_EPS)
    return c * inv, inv


def norm_back(d_norm, x_hat, inv, gain):
    d_hat = d_norm * gain
    m1 = jnp.mean(d_hat, axis=-1, keepdims=True)
    m2 = jnp.mean(d_hat * x_hat, axis=-1, keepdims=True)
    return inv * (d_hat - m1 - x_hat * m2)


def rows_sum(x):
    return jnp.sum(x, axis=0, keepdims=True)


MATS = (('wp', SUB, PX), ('pt', SUB, PPOS), ('qkv', SUB, QKV3), ('out', SUB, D), ('fc', SUB, FF), ('proj', SUBF, D))
NMAT = len(MATS)
VEC = NMAT


def step_kernel(patches, keep, gh_in, w_patch, pos, w_qkv, w_out, w_fc, w_proj, *rest):
    vec_in = rest[:12]
    (h1_out, o_wp, o_pt, o_qkv, o_out, o_fc, o_proj, o_vec) = rest[12:20]
    (kb, z_s, oh_s, wwp, wpt, wqkv, wout, wfc, wproj, vg, v384, vqkv, vfc,
     hat_p, hat_1, hat_2, inv_p, inv_1, inv_2, h_s, a_s, qkv_s, p_s, ctx_s, c_s, gel_s, dpre_s, gh_s, dmid_s, dmb_s, dctx_s, dqkv_s, deb_s,
     gv384, gvqkv, gvfc) = rest[20:56]
    grads = rest[56:63]
    sibs = rest[63:70]
    rds = rest[70:77]
    rss = rest[77:84]
    rfs = rest[84:91]
    g_send, g_recv, r_send, r_recv = rest[91:95]
    outs = (o_wp, o_pt, o_qkv, o_out, o_fc, o_proj, o_vec)

    me = lax.axis_index(AXIS)
    core = lax.rem(me, 2)
    chip = me // 2
    xi = lax.rem(chip, 2)
    yi = chip // 2
    dx = 2 - 4 * xi
    dy = 4 - 8 * yi
    sib = me + 1 - 2 * core
    first = me + dx + core * (dy - dx)
    second = me + dy + core * (dx - dy)
    diag = me + dx + dy

    weights = (wwp, wpt, wqkv, wout, wfc, wproj)
    eye = (lax.broadcasted_iota(jnp.int32, (SUB, SUB), 0) == lax.broadcasted_iota(jnp.int32, (SUB, SUB), 1)).astype(BF16)

    def piece(k, slot):
        if k == VEC:
            return vg.at[slot]
        rows = MATS[k][1]
        return weights[k].at[pl.ds(pl.multiple_of(slot * rows, 16), rows), :]

    def own(k):
        rows = MATS[k][1]
        return pl.ds(pl.multiple_of(me * rows, 16), rows)

    vrow = jnp.zeros((16, 256), F32)
    vg[pl.ds(me, 1)] = vrow.reshape(1, 16, 256)
    for i, ref in enumerate(vec_in):
        width = ref.shape[1]
        vg[pl.ds(me, 1), i:i + 1, 0:width] = ref[...].astype(BF16).astype(F32).reshape(1, 1, width)
    wwp[own(0), :] = dot_nt(eye, w_patch[...].astype(BF16)).astype(BF16)
    wpt[own(1), :] = jnp.zeros((SUB, PPOS), BF16)
    wpt[own(1), 0:NPATCH + 1] = dot_nt(eye, pos[...].astype(BF16)).astype(BF16)
    wqkv[own(2), :] = w_qkv[...].astype(BF16)
    wout[own(3), :] = w_out[...].astype(BF16)
    wfc[own(4), :] = w_fc[...].astype(BF16)
    wproj[own(5), :] = w_proj[...].astype(BF16)

    barrier = pltpu.get_barrier_semaphore()
    for peer in (sib, first, second):
        pl.semaphore_signal(barrier, inc=1, device_id=(peer,), device_id_type=MESH)
    pl.semaphore_wait(barrier, 3)

    def gcopy(k, kind):
        slot, dev = ((me, first), (me, second), (first, second), (me, sib), (first, sib), (second, sib), (diag, sib))[kind]
        return pltpu.make_async_remote_copy(src_ref=piece(k, slot), dst_ref=piece(k, slot), send_sem=g_send.at[k * 7 + kind],
                                            recv_sem=g_recv.at[k * 7 + kind], device_id=(dev,), device_id_type=MESH)

    def gather_start(k):
        gcopy(k, 0).start()
        gcopy(k, 1).start()
        gcopy(k, 3).start()

    def gather_near(k):
        gcopy(k, 0).wait_recv()
        gcopy(k, 2).start()
        gcopy(k, 4).start()
        gcopy(k, 1).wait_recv()
        gcopy(k, 5).start()

    def gather_far(k):
        gcopy(k, 2).wait_recv()
        gcopy(k, 6).start()

    def gather_done(k):
        for kind in (3, 4, 5, 6):
            gcopy(k, kind).wait_recv()

    for k in (0, 1, VEC, 2, 3, 4, 5):
        gather_start(k)

    schip = second // 2
    fchip = first // 2
    dchip = diag // 2

    def rcopy(k, kind):
        g = grads[k]
        src, dst, dev = ((g.at[:, 1 - core], sibs[k], sib), (g.at[dchip, core], rds[k], second),
                         (g.at[schip, core], rss[k], second), (g.at[fchip, core], rfs[k], first))[kind]
        return pltpu.make_async_remote_copy(src_ref=src, dst_ref=dst, send_sem=r_send.at[k * 4 + kind],
                                            recv_sem=r_recv.at[k * 4 + kind], device_id=(dev,), device_id_type=MESH)

    def add_sib(k, c):
        grads[k][c, core] = grads[k][c, core] + sibs[k][c]

    def rs_a(k):
        rcopy(k, 0).start()

    def rs_b(k):
        rcopy(k, 0).wait_recv()
        add_sib(k, dchip)
        add_sib(k, schip)
        rcopy(k, 1).start()
        rcopy(k, 2).start()
        add_sib(k, fchip)
        add_sib(k, chip)

    def rs_c(k):
        rcopy(k, 1).wait_recv()
        grads[k][fchip, core] = grads[k][fchip, core] + rds[k][...]
        rcopy(k, 3).start()

    def rs_d(k):
        rcopy(k, 2).wait_recv()
        rcopy(k, 3).wait_recv()
        outs[k][...] = grads[k][chip, core] + rss[k][...] + rfs[k][...]

    def put(k, val, col=0):
        rows = MATS[k][1]
        width = val.shape[1]
        for o in range(val.shape[0] // rows):
            grads[k][o // 2, o % 2, :, col:col + width] = val[o * rows:(o + 1) * rows, :]

    kb[...] = jnp.full((IMG, 128), -1, jnp.int32)
    kb[:, 0:NKEEP] = keep[...]
    kb[...] = pltpu.roll(kb[...], 1, 1)
    lane = lax.broadcasted_iota(jnp.int32, (1, 128), 1)
    for i in range(IMG):
        kp = jnp.where(lane == 0, 0, kb[i:i + 1, :] + 1)
        kp = jnp.where(lane > NKEEP, -1, kp)
        oh_t = (lax.broadcasted_iota(jnp.int32, (PPOS, 128), 0) == kp).astype(F32)
        oh = oh_t.T[0:TP, :].astype(BF16)
        oh_s[i * TP:(i + 1) * TP, :] = oh
        oh_p = ((lax.broadcasted_iota(jnp.int32, (PPOS, 128), 0) + 1) == kp).astype(F32)
        ohp = oh_p.T[0:TP, 0:NPATCH].astype(BF16)
        z_s[i * TP:(i + 1) * TP, :] = dot(ohp, patches[i]).astype(BF16)
        gh_s[i * TP:(i + 1) * TP, :] = jnp.zeros((TP, D), BF16)
        gh_s[i * TP:i * TP + TOK, :] = gh_in[i]

    gv384[...] = jnp.zeros((16, D), F32)
    gvqkv[...] = jnp.zeros((8, QKV3), F32)
    gvfc[...] = jnp.zeros((8, FF), F32)

    for k in (0, 1, VEC):
        gather_near(k)
    for k in (0, 1, VEC):
        gather_far(k)
    for k in (0, 1, VEC):
        gather_done(k)

    acc_a = jnp.zeros((16, D), F32)
    acc_q = jnp.zeros((8, QKV3), F32)
    acc_f = jnp.zeros((8, FF), F32)
    for d in range(NDEV):
        x = vg[d]
        acc_a += pltpu.roll(jnp.concatenate([x[:, 0:128], jnp.zeros((16, D - 128), F32)], axis=1), SUB * d, 1)
        acc_q += pltpu.roll(jnp.concatenate([x[8:16, :], jnp.zeros((8, QKV3 - 256), F32)], axis=1), (QKV3 // NDEV) * d, 1)
        acc_f += pltpu.roll(jnp.concatenate([x[8:16, :], jnp.zeros((8, FF - 256), F32)], axis=1), SUBF * d, 1)
    v384[...] = acc_a
    vqkv[...] = acc_q
    vfc[...] = acc_f

    def vec(name):
        r = ROW[name]
        return v384[r:r + 1, :]

    def gacc(name, val):
        r = ROW[name]
        gv384[r:r + 1, :] = gv384[r:r + 1, :] + val

    def blocks(body, n=NT // RB, size=RB):
        def step(b, carry):
            body(pl.ds(pl.multiple_of(b * size, size), size))
            return carry
        lax.fori_loop(0, n, step, 0)

    tok_row = lax.rem(lax.broadcasted_iota(jnp.int32, (RB, 1), 0), TP)
    is_cls = tok_row == 0

    def embed(rs):
        e = dot_nt(z_s[rs, :], wwp[...]) + dot_nt(oh_s[rs, :], wpt[...])
        x0 = e + jnp.where(is_cls, vec('cls_tok'), vec('b_patch'))
        xh, inv = norm_stats(x0)
        h0 = xh * vec('lnp_g') + vec('lnp_b')
        hat_p[rs, :] = xh
        inv_p[rs, :] = inv
        h_s[rs, :] = h0
        xh1, inv1 = norm_stats(h0)
        hat_1[rs, :] = xh1
        inv_1[rs, :] = inv1
        a_s[rs, :] = (xh1 * vec('ln1_g') + vec('ln1_b')).astype(BF16)

    blocks(embed)
    gather_near(2)
    gather_far(2)
    gather_done(2)

    def qkv_body(rs):
        qkv_s[rs, :] = (dot(a_s[rs, :], wqkv[...]) + vqkv[2:3, :]).astype(BF16)

    blocks(qkv_body)
    gather_near(3)
    gather_near(4)
    gather_far(3)

    lane_b = lax.broadcasted_iota(jnp.int32, (1, 128), 1)
    lo = (lane_b < HD).astype(F32).astype(BF16)
    hi = (lane_b >= HD).astype(F32).astype(BF16)
    lo_mask = lane_b < HD
    key_ok = lax.broadcasted_iota(jnp.int32, (1, TP, 1), 1) < TOK
    scale = HD ** -0.5

    def att_fwd(i, carry):
        rs = pl.ds(pl.multiple_of(i * TP, TP), TP)
        for j in range(PAIRS):
            cs = slice(j * 128, (j + 1) * 128)
            q = qkv_s[rs, cs]
            k = qkv_s[rs, D + j * 128:D + (j + 1) * 128]
            v = qkv_s[rs, 2 * D + j * 128:2 * D + (j + 1) * 128]
            kk = jnp.concatenate([k * lo, k * hi], axis=0)
            vv = jnp.concatenate([v * lo, v * hi], axis=0)
            s = (dot_nt(kk, q) * scale).reshape(2, TP, TP)
            s = jnp.where(key_ok, s, -jnp.inf)
            e = jnp.exp(s - jnp.max(s, axis=1, keepdims=True))
            p = (e / jnp.sum(e, axis=1, keepdims=True)).reshape(2 * TP, TP)
            p_s[i * PAIRS + j] = p
            ctx_s[rs, cs] = dot_tn(p.astype(BF16), vv).astype(BF16)
        return carry

    lax.fori_loop(0, IMG, att_fwd, 0)
    gather_done(3)
    gather_far(4)
    gather_near(5)

    def out_body(rs):
        hm = h_s[rs, :] + dot(ctx_s[rs, :], wout[...]) + vec('b_out')
        h_s[rs, :] = hm
        xh, inv = norm_stats(hm)
        hat_2[rs, :] = xh
        inv_2[rs, :] = inv
        c_s[rs, :] = (xh * vec('ln2_g') + vec('ln2_b')).astype(BF16)

    blocks(out_body)
    gather_done(4)
    gather_far(5)
    gather_done(5)

    def mlp(rs):
        c = c_s[rs, :]
        gh = gh_s[rs, :]
        for j in range(FF // 512):
            cs = slice(j * 512, (j + 1) * 512)
            u = dot(c, wfc[:, cs]) + vfc[3:4, cs]
            cdf = 0.5 * (1.0 + lax.erf(u * INV_SQRT2))
            gel_s[rs, cs] = (u * cdf).astype(BF16)
            slope = cdf + u * jnp.exp(-0.5 * u * u) * INV_SQRT_2PI
            d_pre = dot_nt(gh, wproj[cs, :]) * slope
            dpre_s[rs, cs] = d_pre.astype(BF16)
            gvfc[3:4, cs] = gvfc[3:4, cs] + rows_sum(d_pre)

    blocks(mlp)

    PROJ, FC, OUT, QKV, WP, PT = 5, 4, 3, 2, 0, 1
    for j in range(FF // 384):
        put_val = dot_tn(gel_s[:, j * 384:(j + 1) * 384], gh_s[...])
        for o in range(2):
            d = j * 2 + o
            grads[PROJ][d // 2, d % 2, :, :] = put_val[o * SUBF:(o + 1) * SUBF, :]
    rs_a(PROJ)
    for j in range(FF // 384):
        put(FC, dot_tn(c_s[...], dpre_s[:, j * 384:(j + 1) * 384]), j * 384)
    rs_a(FC)
    rs_b(PROJ)

    def mid(rs):
        d_c = dot_nt(dpre_s[rs, :], wfc[...])
        xh = hat_2[rs, :]
        gacc('ln2_g', rows_sum(d_c * xh))
        gacc('ln2_b', rows_sum(d_c))
        d_h = gh_s[rs, :].astype(F32)
        gacc('b_proj', rows_sum(d_h))
        d_mid = norm_back(d_c, xh, inv_2[rs, :], vec('ln2_g')) + d_h
        gacc('b_out', rows_sum(d_mid))
        dmid_s[rs, :] = d_mid
        dmb = d_mid.astype(BF16)
        dmb_s[rs, :] = dmb
        dctx_s[rs, :] = dot_nt(dmb, wout[...]).astype(BF16)

    blocks(mid)
    rs_b(FC)
    rs_c(PROJ)
    put(OUT, dot_tn(ctx_s[...], dmb_s[...]))
    rs_a(OUT)

    def att_bwd(i, carry):
        rs = pl.ds(pl.multiple_of(i * TP, TP), TP)
        for j in range(PAIRS):
            cs = slice(j * 128, (j + 1) * 128)
            q = qkv_s[rs, cs]
            k = qkv_s[rs, D + j * 128:D + (j + 1) * 128]
            v = qkv_s[rs, 2 * D + j * 128:2 * D + (j + 1) * 128]
            kk = jnp.concatenate([k * lo, k * hi], axis=0)
            vv = jnp.concatenate([v * lo, v * hi], axis=0)
            dctx = dctx_s[rs, cs]
            p = p_s[i * PAIRS + j]
            dp = dot_nt(vv, dctx)
            t = jnp.sum((p * dp).reshape(2, TP, TP), axis=1, keepdims=True)
            dl = (p * (dp.reshape(2, TP, TP) - t).reshape(2 * TP, TP) * scale).astype(BF16)
            gv2 = dot(p.astype(BF16), dctx)
            gk2 = dot(dl, q)
            g_q = dot_tn(dl, kk)
            g_k = jnp.where(lo_mask, gk2[0:TP, :], gk2[TP:, :])
            g_v = jnp.where(lo_mask, gv2[0:TP, :], gv2[TP:, :])
            for s, g in ((0, g_q), (1, g_k), (2, g_v)):
                c0 = s * D + j * 128
                dqkv_s[rs, c0:c0 + 128] = g.astype(BF16)
                gvqkv[2:3, c0:c0 + 128] = gvqkv[2:3, c0:c0 + 128] + rows_sum(g)
        return carry

    lax.fori_loop(0, IMG // 2, att_bwd, 0)
    rs_b(OUT)
    rs_c(FC)
    lax.fori_loop(IMG // 2, IMG, att_bwd, 0)

    for j in range(3):
        put(QKV, dot_tn(a_s[...], dqkv_s[:, j * 384:(j + 1) * 384]), j * 384)
    rs_a(QKV)
    rs_c(OUT)
    rs_d(PROJ)

    def front(rs):
        d_a = dot_nt(dqkv_s[rs, :], wqkv[...])
        xh1 = hat_1[rs, :]
        gacc('ln1_g', rows_sum(d_a * xh1))
        gacc('ln1_b', rows_sum(d_a))
        d_zero = norm_back(d_a, xh1, inv_1[rs, :], vec('ln1_g')) + dmid_s[rs, :]
        xhp = hat_p[rs, :]
        gacc('lnp_g', rows_sum(d_zero * xhp))
        gacc('lnp_b', rows_sum(d_zero))
        d_x = norm_back(d_zero, xhp, inv_p[rs, :], vec('lnp_g'))
        gacc('cls_tok', rows_sum(jnp.where(is_cls, d_x, 0.0)))
        d_emb = jnp.where(is_cls, 0.0, d_x)
        gacc('b_patch', rows_sum(d_emb))
        deb_s[rs, :] = d_emb.astype(BF16)

    blocks(front)
    rs_b(QKV)
    for j in range(2):
        put(WP, dot_tn(deb_s[...], z_s[:, j * 384:(j + 1) * 384]), j * 384)
    rs_a(WP)
    put(PT, dot_tn(deb_s[...], oh_s[...]))
    rs_a(PT)
    low = (lax.broadcasted_iota(jnp.int32, (8, 256), 0))
    ga = gv384[...]
    gq = gvqkv[...]
    gf = gvfc[...]
    for d in range(NDEV):
        xa = pltpu.roll(ga, (D - SUB * d) % D, 1)[:, 0:256] if d else ga[:, 0:256]
        xq = pltpu.roll(gq, (QKV3 - (QKV3 // NDEV) * d) % QKV3, 1)[:, 0:256] if d else gq[:, 0:256]
        xf = pltpu.roll(gf, (FF - SUBF * d) % FF, 1)[:, 0:256] if d else gf[:, 0:256]
        tail = jnp.where(low == 2, xq, jnp.where(low == 3, xf, xa[8:16, :]))
        grads[VEC][d // 2, d % 2, 0:8, :] = xa[0:8, :]
        grads[VEC][d // 2, d % 2, 8:16, :] = tail
    rs_a(VEC)
    rs_c(QKV)
    rs_d(FC)
    rs_d(OUT)
    rs_b(WP)
    rs_b(PT)
    rs_b(VEC)

    def last(i, carry):
        rs = pl.ds(pl.multiple_of(i * TP, TP), TP)
        h1 = h_s[rs, :] + dot(gel_s[rs, :], wproj[...]) + vec('b_proj')
        h1_out[i] = h1[0:TOK, :].astype(BF16)
        return carry

    lax.fori_loop(0, IMG, last, 0)
    rs_c(WP)
    rs_c(PT)
    rs_c(VEC)
    rs_d(QKV)
    rs_d(WP)
    rs_d(PT)
    rs_d(VEC)
    for k in range(7):
        for kind in range(7):
            gcopy(k, kind).wait_send()
        for kind in range(4):
            rcopy(k, kind).wait_send()


def call_step(args):
    shapes = [(r, c) for _, r, c in MATS] + [(16, 256)]
    vm = lambda s, t: pltpu.VMEM(s, t)
    scratch = [
        vm((IMG, 128), jnp.int32), vm((NT, PX), BF16), vm((NT, PPOS), BF16),
        vm((D, PX), BF16), vm((D, PPOS), BF16), vm((D, QKV3), BF16), vm((D, D), BF16), vm((D, FF), BF16), vm((FF, D), BF16),
        vm((NDEV, 16, 256), F32), vm((16, D), F32), vm((8, QKV3), F32), vm((8, FF), F32),
        vm((NT, D), F32), vm((NT, D), F32), vm((NT, D), F32), vm((NT, 1), F32), vm((NT, 1), F32), vm((NT, 1), F32),
        vm((NT, D), F32), vm((NT, D), BF16), vm((NT, QKV3), BF16), vm((IMG * PAIRS, 2 * TP, TP), F32), vm((NT, D), BF16),
        vm((NT, D), BF16), vm((NT, FF), BF16), vm((NT, FF), BF16), vm((NT, D), BF16), vm((NT, D), F32), vm((NT, D), BF16),
        vm((NT, D), BF16), vm((NT, QKV3), BF16), vm((NT, D), BF16),
        vm((16, D), F32), vm((8, QKV3), F32), vm((8, FF), F32),
    ]
    scratch += [vm((4, 2) + s, F32) for s in shapes]
    scratch += [vm((4,) + s, F32) for s in shapes]
    scratch += [vm(s, F32) for s in shapes] * 3
    scratch += [pltpu.SemaphoreType.DMA((49,)), pltpu.SemaphoreType.DMA((49,)), pltpu.SemaphoreType.DMA((28,)), pltpu.SemaphoreType.DMA((28,))]
    vmem = pl.BlockSpec(memory_space=pltpu.VMEM)
    return pl.pallas_call(
        step_kernel,
        out_shape=[jax.ShapeDtypeStruct((IMG, TOK, D), BF16)] + [jax.ShapeDtypeStruct(s, F32) for s in shapes],
        in_specs=[vmem] * len(args),
        out_specs=[vmem] * 8,
        scratch_shapes=scratch,
        compiler_params=pltpu.CompilerParams(collective_id=0, has_side_effects=True, vmem_limit_bytes=67043328),
        name='vit_step',
    )(*args)


def solution(mesh):
    def spec_of(name):
        return P(None, AXIS) if name in LAST_SPLIT else P(AXIS)

    def local_step(patches, keep, *rest):
        w = dict(zip(PARAM_NAMES, rest[:-1]))
        args = [patches, keep, rest[-1], w['w_patch'], w['pos_table'], w['w_qkv'].reshape(SUB, QKV3), w['w_out'], w['w_fc'], w['w_proj']]
        args += [w[name].reshape(1, -1) for name in VROWS]
        h1, g_wp, g_pt, g_qkv, g_out, g_fc, g_proj, g_vec = call_step(args)
        width = {'b_qkv': QKV3 // NDEV, 'b_fc': SUBF}
        g = {name: g_vec[ROW[name], :width.get(name, SUB)] for name in VROWS}
        g['w_patch'] = g_wp.T
        g['pos_table'] = jnp.concatenate([g['cls_tok'][None], g_pt[:, 1:NPATCH + 1].T], axis=0)
        g['w_qkv'] = g_qkv.reshape(SUB, 3, 6, HD)
        g['w_out'] = g_out
        g['w_fc'] = g_fc
        g['w_proj'] = g_proj
        return (h1,) + tuple(g[name] for name in PARAM_NAMES)

    batch_spec = P(AXIS)
    param_specs = tuple(spec_of(name) for name in PARAM_NAMES)
    return jax.shard_map(local_step, mesh=mesh, in_specs=(batch_spec, batch_spec) + param_specs + (batch_spec,), out_specs=(batch_spec,) + param_specs, check_vma=False)
```

time: 463 us -> 123 us (0.27); the launches traced: 455 us -> 123 us
  blocking collectives: 156 us -> 0 us
  waiting for transfers between devices: 145 us -> 0 us
  Pallas kernels: 0 us -> 100 us
  matrix products: 77.6 us -> 0 us
  other arithmetic: 40.5 us -> 0.71 us
  between operations: 15.4 us -> 0.72 us
    reduce_scatter x5 -> x0, waiting for transfers between devices: 145 us -> none  [local_step(): lax.psum_scatter(grad_map[name], MESH_AXIS, scatter_dimension=split_of(na...]
    pallas_call x0 -> x1, Pallas kernels: none -> 100 us  [call_step(): pl.pallas_call(step_kernel, out_shape=[jax.ShapeDtypeStruct((IMG, TOK, D)...]
    all_gather x6 -> x0, blocking collectives: 85.1 us -> none  [gather_whole(): lax.all_gather(shard.astype(jnp.bfloat16), MESH_AXIS, axis=split_of(name)...]
    dot_general x23 -> x0, matrix products: 77.6 us -> none  [product(): jnp.einsum(einsum_form, left_op, right_op, preferred_element_type=jnp.flo...]
    unnamed x3 -> x0, blocking collectives: 70.9 us -> none
    convert_element_type x40 -> x0, other arithmetic: 27.1 us -> none  [the longest x25 14.5 us: gather_whole(): shard.astype(jnp.bfloat16)]
    reduce_sum x10 -> x0, other arithmetic: 9.79 us -> none  [the longest x1 3.04 us: backward(): jnp.sum(d_qkv, axis=(0, 1)).reshape(-1)]
    unnamed x116 -> x21, local copies, waits for them, and re-layouts: 20.2 us -> 14.2 us
  transfers between devices with their start and end apart: 10 -> 0, of which waited for: 4 -> 0; matrix products, arithmetic and copies ran while one was open for 19% -> 0% of each run, Pallas kernels for 0% -> 0%
where the time goes in v1:
time: 123 us
  Pallas kernels  100 us (81%)
  local copies, waits for them, and re-layouts  21.1 us (17%)
    pallas_call x1, Pallas kernels, call_step(): pl.pallas_call(step_kernel, out_shape=[jax.ShapeDtypeStruct((IMG, TOK, D)...  100 us
    unnamed x21, local copies, waits for them, and re-layouts  14.2 us
    slice x3, local copies, waits for them, and re-layouts, local_step(): g = {name: g_vec[ROW[name], :width.get(name, SUB)] for name in VROWS}  2.61 us

profile of v1, /device:TPU:0, one launch (start us, length us, event | category | flops | bytes accessed | tf_op | source)
XLA Modules:
  0.0 122.7 jit_solution(17024688869434528482)
XLA Ops:
  0.7 0.0 copy-start
  0.7 1.7 %copy.52.pos = f32[197,48]{1,0:T(8,128)} copy(f32[197,48]{0,1:T(8,128)} %param.25) | data formatting | bytes 75648 | tf_op args[4]
  2.4 1.8 %copy.51.w_patch = f32[768,48]{1,0:T(8,128)} copy(f32[768,48]{0,1:T(8,128)} %param.23) | data formatting | bytes 294912 | tf_op args[2]
  4.2 1.2 copy.48
  5.3 0.8 reshape.80.w_qkv
  6.2 2.0 %copy.50.gh_in = bf16[8,99,384]{2,1,0:T(8,128)(2,1)} copy(bf16[8,99,384]{2,0,1:T(8,128)(2,1)} %param.41) | data formatting | bytes 1216512 | tf_op args[20]
  8.2 0.0 copy-done
  8.2 1.9 %copy.49.patches = bf16[8,196,768]{2,1,0:T(8,128)(2,1)} copy(bf16[8,196,768]{2,0,1:T(8,128)(2,1)S(1)} %copy-done) | data formatting | bytes 4816896 | tf_op args[0]
  10.1 100.2 %vit_step.1 = (bf16[8,99,384]{2,1,0:T(8,128)(2,1)}, f32[48,768]{1,0:T(8,128)}, f32[48,256]{1,0:T(8,128)}, f32[48,1152]{1,0:T(8,128)}, f32[48,384]{1,0:T(8,128)},...) custom-call(bf16[8,196,768]{2,1,0:T(8,128)(2,1)} %copy.49.patches, s32[8,98]{1,0:T(8,128)} %keep.1, ...), custom_call_target="tpu_custom_call" | custom-call | tf_op jit(solution)/shard_map/vit_step/pallas_call | solution.py:490
  110.3 0.0 copy-start.3
  110.3 0.0 copy-start.4
  110.3 0.0 copy-start.2
  110.3 0.0 copy-start.1
  110.4 2.0 %copy.54 = bf16[8,99,384]{2,0,1:T(8,128)(2,1)} copy(bf16[8,99,384]{2,1,0:T(8,128)(2,1)} %get-tuple-element.54) | data formatting | bytes 1216512
  112.4 1.3 %slice.50 = f32[1,192]{1,0:T(1,128)} slice(f32[16,256]{1,0:T(8,128)} %get-tuple-element.29), slice={[11:12], [0:192]} | slice | bytes 1536 | tf_op jit(solution)/shard_map/slice | solution.py:511
  113.7 1.3 %slice.46 = f32[1,144]{1,0:T(1,128)} slice(f32[16,256]{1,0:T(8,128)} %get-tuple-element.29), slice={[10:11], [0:144]} | slice | bytes 1152 | tf_op jit(solution)/shard_map/slice | solution.py:511
  114.9 1.5 %slice_bitcast_fusion.1 = (f32[48]{0:T(128)}, f32[48]{0:T(128)}, f32[48]{0:T(128)}, f32[48]{0:T(128)}, f32[48]{0:T(128)}, /*index=5*/f32[48]{0:T(128)}, f32[48]{...) fusion(f32[16,256]{1,0:T(8,128)} %get-tuple-element.29), kind=kLoop, calls=%fused_computation.2 | loop fusion | bytes 4032 | tf_op jit(solution)/shard_map/squeeze | solution.py:511
  116.4 0.1 copy.53
  116.5 0.9 slice_bitcast_fusion
  117.4 0.7 pad_maximum_fusion
  118.1 1.1 reshape.93
  119.2 0.8 copy.55
  120.0 0.0 copy-done.3
  120.0 0.7 copy.60
  120.7 0.0 copy-done.4
  120.7 0.6 copy.61
  121.3 0.0 copy-done.2
  121.3 0.7 copy.62
  122.0 0.0 copy-done.1
  122.0 0.7 copy.63
Async XLA Ops:
  0.7 7.5 %copy-start = (bf16[8,196,768]{2,0,1:T(8,128)(2,1)S(1)}, bf16[8,196,768]{2,0,1:T(8,128)(2,1)}, u32[]{:S(2)}) copy-start(bf16[8,196,768]{2,0,1:T(8,128)(2,1)} %param.21) | copy-start | bytes 7225348
  110.3 9.7 %copy-start.3 = (f32[48,768]{1,0:T(8,128)S(1)}, f32[48,768]{1,0:T(8,128)}, u32[]{:S(2)}) copy-start(f32[48,768]{1,0:T(8,128)} %get-tuple-element.28) | copy-start | bytes 442372
  110.3 10.4 %copy-start.4 = (f32[48,384]{1,0:T(8,128)S(1)}, f32[48,384]{1,0:T(8,128)}, u32[]{:S(2)}) copy-start(f32[48,384]{1,0:T(8,128)} %get-tuple-element.114) | copy-start | bytes 221188
  110.3 11.0 %copy-start.2 = (f32[48,1536]{1,0:T(8,128)S(1)}, f32[48,1536]{1,0:T(8,128)}, u32[]{:S(2)}) copy-start(f32[48,1536]{1,0:T(8,128)} %get-tuple-element.118) | copy-start | bytes 884740
  110.3 11.7 %copy-start.1 = (f32[192,384]{1,0:T(8,128)S(1)}, f32[192,384]{1,0:T(8,128)}, u32[]{:S(2)}) copy-start(f32[192,384]{1,0:T(8,128)} %get-tuple-element.120) | copy-start | bytes 884740
